TPU v7x, 32 devices: a whole 2x2x4 slice. The times are simulated.
32 devices in a mesh: tm: 4 (over y, x), paths: 8 (over z, core).
Axes of the slice: x: 2, y: 2, z: 4, core: 2. Of those that a mesh axis runs over, the one named last changes fastest.
Arguments:
- returns: bfloat16 [128, 4096, 256], P('tm', 'paths'), may hold values from -0.15917969 to 0.15917969
- weights: bfloat16 [256, 64], P('paths'), may hold values from -0.375 to 0.375
Outputs:
- drawdown: float32 [64, 4096], P('tm', 'paths')
All inputs are finite; a program needn't handle non-finite values.
Results may differ from a plain program's by a relative error of at most 0.0003.
Values may be sent and summed in bfloat16 or wider, within the bound.
A program may use at most 64 MiB of HBM per device.

v0:
```python
import jax
import jax.numpy as jnp
from jax import lax
from jax.sharding import PartitionSpec as P

very_large = 1e30


def prefix(part, axis, combine, identity):
    place = lax.axis_index(axis)
    gathered = jax.tree.map(lambda a: lax.all_gather(a, axis), part)
    state = jax.tree.map(lambda a, e: jnp.zeros_like(a) + jnp.asarray(e, a.dtype), part, identity)

    def one(lap, state):
        return combine(
            state, jax.tree.map(lambda a: lax.dynamic_index_in_dim(a, lap, 0, False), gathered)
        )

    return lax.fori_loop(0, place, one, state)


def join_two(earlier, later):
    return (earlier[0] + later[0], jnp.maximum(earlier[1], earlier[0] + later[1]))


def shards(returns, weights):
    all_weights = lax.all_gather(weights, "paths", axis=0, tiled=True)
    profit = jnp.einsum("tpa,aq->tqp", returns, all_weights, preferred_element_type=jnp.float32)
    steps_here = profit.shape[0]
    row_ids = lax.broadcasted_iota(jnp.int32, (steps_here, steps_here), 0)
    col_ids = lax.broadcasted_iota(jnp.int32, (steps_here, steps_here), 1)
    lower = (row_ids >= col_ids).astype(jnp.float32)
    flat = profit.reshape(steps_here, -1)
    values = jnp.dot(
        lower, flat, precision=lax.Precision.HIGHEST, preferred_element_type=jnp.float32
    ).reshape(profit.shape)
    peaks = jnp.maximum(lax.cummax(values, axis=0), 0.0)
    offset = values[-1]
    highest = peaks[-1]
    segments = lax.axis_size("tm")
    block_width = offset.shape[0] // segments
    zeros = jnp.zeros_like(offset)
    prior_offset, prior_peak = prefix(
        (offset, highest), "tm", join_two, (zeros, zeros - very_large)
    )
    running = jnp.maximum(prior_peak[None], prior_offset[None] + peaks)
    falls = jnp.max(running - (prior_offset[None] + values), axis=0)
    blocks = falls.reshape(segments, block_width, falls.shape[1])
    received = lax.all_to_all(blocks, "tm", split_axis=0, concat_axis=0, tiled=True)
    return jnp.max(received, axis=0)


def solution(mesh):
    in_specs = (P("tm", "paths", None), P("paths", None))
    out_specs = P("tm", "paths")
    return jax.shard_map(shards, mesh=mesh, in_specs=in_specs, out_specs=out_specs, check_vma=False)
```

profile of v0, /device:TPU:0, one launch (start us, length us, event | category | flops | bytes accessed | tf_op | source)
XLA Modules:
  0.0 87.8 jit_solution(8947005105098982368)
XLA Ops:
  0.0 15.9 %all_gather.9 = bf16[256,64]{1,0:T(8,128)(2,1)S(1)} all-gather(bf16[32,64]{1,0:T(8,128)(2,1)} %param.5), channel_id=1, replica_groups=mesh['tm'=4,'paths'=8] {'paths'}, dimensions={0}, use_global_device_ids=true | all-gather | bytes 36864 | tf_op jit(solution)/shard_map/all_gather | solution.py:27
  15.9 6.0 %fusion.1 = f32[64,32,512]{2,0,1:T(8,128)S(1)} fusion(bf16[32,512,256]{2,1,0:T(8,128)(2,1)} %param.4, bf16[256,64]{1,0:T(8,128)(2,1)S(1)} %all_gather.9), kind=kOutput, calls=%fused_computation.6 | convolution fusion | flops 536870912 | bytes 12615680 | tf_op jit(solution)/shard_map/tpa,aq->tqp/dot_general | solution.py:28
  21.9 2.4 %copy.3 = f32[4,8,64,512]{3,1,2,0:T(8,128)S(1)} copy(f32[4,8,64,512]{3,2,1,0:T(8,128)S(1)} %bitcast.27) | data formatting | bytes 8388608
  24.4 2.1 %fusion.3 = f32[32,32768]{1,0:T(8,128)S(1)} fusion(f32[32,32768]{1,0:T(8,128)S(1)} %bitcast.29), kind=kOutput, calls=%fused_computation.9 | convolution fusion | flops 402654208 | bytes 8388608 | tf_op jit(solution)/shard_map/dot_general | solution.py:34
  26.5 0.0 copy-start
  26.5 0.4 slice_reduce_fusion
  26.9 2.4 %copy.4 = f32[4,8,64,512]{3,2,1,0:T(8,128)S(1)} copy(f32[4,8,64,512]{3,1,2,0:T(8,128)S(1)} %bitcast.25) | data formatting | bytes 8388608
  29.3 0.0 copy-done
  29.3 20.9 %broadcast_maximum_fusion = f32[32,64,512]{2,1,0:T(8,128)S(1)} fusion(f32[32,64,512]{2,1,0:T(8,128)S(1)} %bitcast.30), kind=kOutput, calls=%fused_computation.4 | output fusion | flops 33554432 | bytes 8388608 | tf_op jit(solution)/shard_map/shards/reduce_window_max | solution.py:37
  50.2 0.0 copy-start.2
  50.2 2.0 %copy-done.2 = f32[32,64,512]{2,1,0:T(8,128)} copy-done((f32[32,64,512]{2,1,0:T(8,128)}, f32[32,64,512]{2,1,0:T(8,128)S(1)}, u32[]{:S(2)}) %copy-start.2) | copy-done | bytes 4194328
  52.2 10.3 %all_gather.11 = f32[4,64,512]{2,1,0:T(8,128)S(1)} all-gather(f32[1,64,512]{2,1,0:T(8,128)S(1)} %slice.13), channel_id=1, replica_groups=mesh['tm'=4,'paths'=8] {'tm'}, dimensions={0}, use_global_device_ids=true | all-gather | bytes 655360 | tf_op jit(solution)/shard_map/all_gather | solution.py:11
  62.6 10.7 %all_gather.10 = f32[4,64,512]{2,1,0:T(8,128)S(1)} all-gather(f32[1,64,512]{2,1,0:T(8,128)S(1)} %slice.10), channel_id=1, replica_groups=mesh['tm'=4,'paths'=8] {'tm'}, dimensions={0}, use_global_device_ids=true | all-gather | bytes 655360 | tf_op jit(solution)/shard_map/all_gather | solution.py:11
  73.3 0.2 while.12
  73.6 0.0 copy-start.1
  73.6 4.8 %copy.7 = f32[4,8,64,512]{3,1,2,0:T(8,128)S(1)} copy(f32[4,8,64,512]{3,2,1,0:T(8,128)} %bitcast.26) | data formatting | bytes 8388608
  78.4 0.0 copy-done.1
  78.4 0.9 %subtract_reduce_fusion = f32[32768]{0:T(1024)S(1)} fusion(f32[32,32768]{1,0:T(8,128)S(1)} %copy-done.1, f32[32,32768]{1,0:T(8,128)S(1)} %bitcast.28, f32[32768]{0:T(1024)S(1)} %bitcast.33, f32[32768]{0:T(1024)S(1)} %bitcast.34), kind=kLoop, calls=%fused_computation.3 | loop fusion | flops 5210112 | bytes 8781824 | tf_op jit(solution)/shard_map/reduce_max | solution.py:47
  79.4 7.8 %all_to_all.5 = f32[4,16,512]{2,1,0:T(8,128)S(1)} all-to-all(f32[4,16,512]{2,1,0:T(8,128)S(1)} %reshape.24), channel_id=1, replica_groups=mesh['tm'=4,'paths'=8] {'tm'}, dimensions={0} | all-to-all | bytes 262144 | tf_op jit(solution)/shard_map/all_to_all | solution.py:49
  87.2 0.6 reduce_max.19
  (7 shorter events, 0.1 us)
Async XLA Ops:
  26.5 2.8 %copy-start = (f32[32,32768]{1,0:T(8,128)}, f32[32,32768]{1,0:T(8,128)S(1)}, u32[]{:S(2)}) copy-start(f32[32,32768]{1,0:T(8,128)S(1)} %fusion.3) | copy-start | bytes 12582916
  50.2 2.0 %copy-start.2 = (f32[32,64,512]{2,1,0:T(8,128)}, f32[32,64,512]{2,1,0:T(8,128)S(1)}, u32[]{:S(2)}) copy-start(f32[32,64,512]{2,1,0:T(8,128)S(1)} %broadcast_maximum_fusion) | copy-start | bytes 12582916
  73.6 4.8 %copy-start.1 = (f32[32,32768]{1,0:T(8,128)S(1)}, f32[32,32768]{1,0:T(8,128)}, u32[]{:S(2)}) copy-start(f32[32,32768]{1,0:T(8,128)} %copy-done) | copy-start | bytes 12582916
where the time goes:
time: 88.1 us; the launch traced here: 87.8 us
  blocking collectives  44.8 us (51%)
  other arithmetic  22.5 us (26%)
  local copies, waits for them, and re-layouts  12.1 us (14%)
  matrix products  8.14 us (9%)
    all_gather x2, blocking collectives, prefix(): gathered = jax.tree.map(lambda a: lax.all_gather(a, axis), part)  21 us
    another operation x1, other arithmetic, shards(): peaks = jnp.maximum(lax.cummax(values, axis=0), 0.0)  20.9 us
    all_gather x1, blocking collectives, shards(): all_weights = lax.all_gather(weights, 'paths', axis=0, tiled=True)  15.9 us
    unnamed x11, local copies, waits for them, and re-layouts  11.7 us
    all_to_all x1, blocking collectives, shards(): lax.all_to_all(blocks, 'tm', split_axis=0, concat_axis=0, tiled=True)  7.85 us
    dot_general x1, matrix products, shards(): jnp.einsum('tpa,aq->tqp', returns, all_weights, preferred_element_type=jn...  6.03 us
    dot_general x1, matrix products, shards(): jnp.dot(lower, flat, precision=lax.Precision.HIGHEST, preferred_element_t...  2.11 us

commit v1 on v0

--- a/solution.py
+++ b/solution.py
@@ -24,8 +24,25 @@
 
 
 def shards(returns, weights):
-    all_weights = lax.all_gather(weights, "paths", axis=0, tiled=True)
-    profit = jnp.einsum("tpa,aq->tqp", returns, all_weights, preferred_element_type=jnp.float32)
+    size, here = (lax.axis_size("paths"), lax.axis_index("paths"))
+    behind = [(i, (i - 1) % size) for i in range(size)]
+    width = weights.shape[0]
+    held = weights
+    total = jnp.einsum(
+        "tpa,aq->tqp",
+        lax.dynamic_slice_in_dim(returns, here * width, held.shape[0], axis=2),
+        held,
+        preferred_element_type=jnp.float32,
+    )
+    for step in range(1, size):
+        held = lax.ppermute(held, "paths", behind)
+        total = total + jnp.einsum(
+            "tpa,aq->tqp",
+            lax.dynamic_slice_in_dim(returns, (here + step) % size * width, held.shape[0], axis=2),
+            held,
+            preferred_element_type=jnp.float32,
+        )
+    profit = total
     steps_here = profit.shape[0]
     row_ids = lax.broadcasted_iota(jnp.int32, (steps_here, steps_here), 0)
     col_ids = lax.broadcasted_iota(jnp.int32, (steps_here, steps_here), 1)

time: 88.1 us -> 120 us (1.36)
  matrix products: 8.14 us -> 42.5 us
  blocking collectives: 44.8 us -> 28.6 us
  starting transfers between devices: 0 us -> 11.5 us
  local copies, waits for them, and re-layouts: 12.1 us -> 14.3 us
    dot_general x1 -> x8, matrix products: 6.03 us -> 40.4 us  [the longest x7 34.9 us: shards(): jnp.einsum('tpa,aq->tqp', lax.dynamic_slice_in_dim(returns, (here + step)...]
    all_gather x1 -> x0, blocking collectives: 15.9 us -> none  [shards(): all_weights = lax.all_gather(weights, 'paths', axis=0, tiled=True)]
    ppermute x0 -> x7, starting transfers between devices: none -> 11.5 us  [shards(): held = lax.ppermute(held, 'paths', behind)]
    unnamed x11 -> x13, local copies, waits for them, and re-layouts: 11.7 us -> 13.9 us
  transfers between devices with their start and end apart: 0 -> 7, of which waited for: 0 -> 0; matrix products, arithmetic and copies ran while one was open for 0% -> 23% of each run, Pallas kernels for 0% -> 0%
where the time goes in v1:
time: 120 us
  matrix products  42.5 us (35%)
  blocking collectives  28.6 us (24%)
  other arithmetic  22.5 us (19%)
  local copies, waits for them, and re-layouts  14.3 us (12%)
  starting transfers between devices  11.5 us (10%)
    dot_general x7, matrix products, shards(): jnp.einsum('tpa,aq->tqp', lax.dynamic_slice_in_dim(returns, (here + step)...  34.9 us
    another operation x1, other arithmetic, shards(): peaks = jnp.maximum(lax.cummax(values, axis=0), 0.0)  20.9 us
    all_gather x2, blocking collectives, prefix(): gathered = jax.tree.map(lambda a: lax.all_gather(a, axis), part)  20.8 us
    unnamed x13, local copies, waits for them, and re-layouts  13.9 us
    ppermute x7, starting transfers between devices, shards(): held = lax.ppermute(held, 'paths', behind)  11.5 us
    all_to_all x1, blocking collectives, shards(): lax.all_to_all(blocks, 'tm', split_axis=0, concat_axis=0, tiled=True)  7.85 us
    dot_general x1, matrix products, shards(): jnp.einsum('tpa,aq->tqp', lax.dynamic_slice_in_dim(returns, here * width,...  5.46 us
  transfers between devices with their start and end apart: 7, of which 0 were waited for; matrix products, arithmetic and copies ran while one was open for 23% of the time, Pallas kernels for 0%

profile of v1, /device:TPU:0, one launch (start us, length us, event | category | flops | bytes accessed | tf_op | source)
XLA Modules:
  0.0 119.8 jit_solution(18070147842172265604)
XLA Ops:
  0.0 4.5 %collective-permute-start = (bf16[32,64]{1,0:T(8,128)(2,1)}, bf16[32,64]{1,0:T(8,128)(2,1)S(1)}, u32[]{:S(2)}, u32[]{:S(2)}) collective-permute-start(bf16[32,64]{1,0:T(8,128)(2,1)} %param.5), channel_id=1, source_target_pairs={{0,7},{1,0},{2,1},{3,2},{4,3},{5,4},{6,5},{7,6},{8,15},{9,8},{10,9... | collective-permute-start | bytes 12296 | tf_op jit(solution)/shard_map/ppermute | solution.py:38
  4.5 5.5 %fusion.15 = f32[32,512,64]{1,2,0:T(8,128)} fusion(bf16[32,512,256]{2,1,0:T(8,128)(2,1)} %param.4, s32[]{:T(128)S(6)} %select_n.60, bf16[32,64]{1,0:T(8,128)(2,1)} %param.5), kind=kOutput, calls=%fused_computation.19 | convolution fusion | flops 67108864 | bytes 8396804 | tf_op jit(solution)/shard_map/tpa,aq->tqp/dot_general | solution.py:31
  10.0 0.0 copy-start
  10.0 0.0 collective-permute-done
  10.0 0.7 collective-permute-start.1
  10.7 5.8 %fusion.13 = f32[32,512,64]{1,2,0:T(8,128)} fusion(bf16[32,512,256]{2,1,0:T(8,128)(2,1)} %param.4, s32[]{:T(128)S(6)} %select_n.62, bf16[32,64]{1,0:T(8,128)(2,1)S(1)} %collective-permute-done), kind=kOutput, calls=%fused_computation.17 | convolution fusion | flops 67108864 | bytes 8392708 | tf_op jit(solution)/shard_map/tpa,aq->tqp/dot_general | solution.py:39
  16.4 0.0 collective-permute-done.1
  16.4 0.0 collective-permute-start.2
  16.4 0.0 copy-done
  16.4 3.3 %fusion.11 = f32[32,512,64]{1,2,0:T(8,128)} fusion(bf16[32,512,256]{2,1,0:T(8,128)(2,1)S(1)} %copy-done, s32[]{:T(128)S(6)} %select_n.64, bf16[32,64]{1,0:T(8,128)(2,1)S(1)} %collective-permute-done.1), kind=kOutput, calls=%fused_computation.15 | convolution fusion | flops 67108864 | bytes 8396804 | tf_op jit(solution)/shard_map/tpa,aq->tqp/dot_general | solution.py:39
  19.7 0.0 collective-permute-done.2
  19.7 1.6 %collective-permute-start.3 = (bf16[32,64]{1,0:T(8,128)(2,1)S(1)}, bf16[32,64]{1,0:T(8,128)(2,1)S(1)}, u32[]{:S(2)}, u32[]{:S(2)}) collective-permute-start(bf16[32,64]{1,0:T(8,128)(2,1)S(1)} %collective-permute-done.2), channel_id=1, source_target_pairs={{0,7},{1,0},{2,1},{3,2},{4,3},{5,4},{6,5},{7,6},{8,15},{9,8},{10,9... | collective-permute-start | bytes 12296 | tf_op jit(solution)/shard_map/ppermute | solution.py:38
  21.3 3.3 %fusion.9 = f32[32,512,64]{1,2,0:T(8,128)} fusion(bf16[32,512,256]{2,1,0:T(8,128)(2,1)S(1)} %copy-done, s32[]{:T(128)S(6)} %select_n.66, bf16[32,64]{1,0:T(8,128)(2,1)S(1)} %collective-permute-done.2), kind=kOutput, calls=%fused_computation.13 | convolution fusion | flops 67108864 | bytes 8396804 | tf_op jit(solution)/shard_map/tpa,aq->tqp/dot_general | solution.py:39
  24.6 0.0 collective-permute-done.3
  24.6 1.6 %collective-permute-start.4 = (bf16[32,64]{1,0:T(8,128)(2,1)S(1)}, bf16[32,64]{1,0:T(8,128)(2,1)S(1)}, u32[]{:S(2)}, u32[]{:S(2)}) collective-permute-start(bf16[32,64]{1,0:T(8,128)(2,1)S(1)} %collective-permute-done.3), channel_id=1, source_target_pairs={{0,7},{1,0},{2,1},{3,2},{4,3},{5,4},{6,5},{7,6},{8,15},{9,8},{10,9... | collective-permute-start | bytes 12296 | tf_op jit(solution)/shard_map/ppermute | solution.py:38
  26.2 3.3 %fusion.7 = f32[32,512,64]{1,2,0:T(8,128)} fusion(bf16[32,512,256]{2,1,0:T(8,128)(2,1)S(1)} %copy-done, s32[]{:T(128)S(6)} %select_n.68, bf16[32,64]{1,0:T(8,128)(2,1)S(1)} %collective-permute-done.3), kind=kOutput, calls=%fused_computation.11 | convolution fusion | flops 67108864 | bytes 8396804 | tf_op jit(solution)/shard_map/tpa,aq->tqp/dot_general | solution.py:39
  29.5 0.0 collective-permute-done.4
  29.5 1.6 %collective-permute-start.5 = (bf16[32,64]{1,0:T(8,128)(2,1)S(1)}, bf16[32,64]{1,0:T(8,128)(2,1)S(1)}, u32[]{:S(2)}, u32[]{:S(2)}) collective-permute-start(bf16[32,64]{1,0:T(8,128)(2,1)S(1)} %collective-permute-done.4), channel_id=1, source_target_pairs={{0,7},{1,0},{2,1},{3,2},{4,3},{5,4},{6,5},{7,6},{8,15},{9,8},{10,9... | collective-permute-start | bytes 12296 | tf_op jit(solution)/shard_map/ppermute | solution.py:38
  31.1 3.3 %fusion.5 = f32[32,512,64]{1,2,0:T(8,128)} fusion(bf16[32,512,256]{2,1,0:T(8,128)(2,1)S(1)} %copy-done, s32[]{:T(128)S(6)} %select_n.70, bf16[32,64]{1,0:T(8,128)(2,1)S(1)} %collective-permute-done.4), kind=kOutput, calls=%fused_computation.9 | convolution fusion | flops 67108864 | bytes 8396804 | tf_op jit(solution)/shard_map/tpa,aq->tqp/dot_general | solution.py:39
  34.4 0.0 collective-permute-done.5
  34.4 1.6 %collective-permute-start.6 = (bf16[32,64]{1,0:T(8,128)(2,1)S(1)}, bf16[32,64]{1,0:T(8,128)(2,1)S(1)}, u32[]{:S(2)}, u32[]{:S(2)}) collective-permute-start(bf16[32,64]{1,0:T(8,128)(2,1)S(1)} %collective-permute-done.5), channel_id=1, source_target_pairs={{0,7},{1,0},{2,1},{3,2},{4,3},{5,4},{6,5},{7,6},{8,15},{9,8},{10,9... | collective-permute-start | bytes 12296 | tf_op jit(solution)/shard_map/ppermute | solution.py:38
  35.9 3.3 %fusion.3 = f32[32,512,64]{1,2,0:T(8,128)} fusion(bf16[32,512,256]{2,1,0:T(8,128)(2,1)S(1)} %copy-done, s32[]{:T(128)S(6)} %select_n.72, bf16[32,64]{1,0:T(8,128)(2,1)S(1)} %collective-permute-done.5), kind=kOutput, calls=%fused_computation.7 | convolution fusion | flops 67108864 | bytes 8396804 | tf_op jit(solution)/shard_map/tpa,aq->tqp/dot_general | solution.py:39
  39.2 0.0 collective-permute-done.6
  39.2 12.7 %add_add_fusion = f32[32,512,64]{1,2,0:T(8,128)} fusion(f32[32,512,64]{1,2,0:T(8,128)} %fusion.3, f32[32,512,64]{1,2,0:T(8,128)} %fusion.5, f32[32,512,64]{1,2,0:T(8,128)} %fusion.7, f32[32,512,64]{1,2,0:T(8,128)} %fusion.9, f32[32,512,64]{1,2,0:T(8,128)} %fusion.11, f32[32,512,64]{1,2,0:T(8,128)} %fusion.15, f32[32,512,64]{1,2,0:T(8,128)} %fusion.13, ...), kind=kOutput, calls=%fused_computation.3 | convolution fusion | flops 74448896 | bytes 37756932 | tf_op jit(solution)/shard_map/tpa,aq->tqp/dot_general | solution.py:39
  52.0 4.6 %copy.35 = f32[4,8,64,512]{3,1,2,0:T(8,128)S(1)} copy(f32[4,8,64,512]{3,2,1,0:T(8,128)} %bitcast.50) | data formatting | bytes 8388608
  56.6 2.1 %fusion.19 = f32[32,32768]{1,0:T(8,128)S(1)} fusion(f32[32,32768]{1,0:T(8,128)S(1)} %bitcast.48), kind=kOutput, calls=%fused_computation.24 | convolution fusion | flops 402654208 | bytes 8388608 | tf_op jit(solution)/shard_map/dot_general | solution.py:51
  58.7 0.0 copy-start.1
  58.7 0.4 slice_reduce_fusion
  59.1 2.4 %copy.36 = f32[4,8,64,512]{3,2,1,0:T(8,128)S(1)} copy(f32[4,8,64,512]{3,1,2,0:T(8,128)S(1)} %bitcast.45) | data formatting | bytes 8388608
  61.5 0.0 copy-done.1
  61.5 20.9 %broadcast_maximum_fusion = f32[32,64,512]{2,1,0:T(8,128)S(1)} fusion(f32[32,64,512]{2,1,0:T(8,128)S(1)} %bitcast.49), kind=kOutput, calls=%fused_computation.21 | output fusion | flops 33554432 | bytes 8388608 | tf_op jit(solution)/shard_map/shards/reduce_window_max | solution.py:54
  82.5 0.0 copy-start.3
  82.5 2.0 %copy-done.3 = f32[32,64,512]{2,1,0:T(8,128)} copy-done((f32[32,64,512]{2,1,0:T(8,128)}, f32[32,64,512]{2,1,0:T(8,128)S(1)}, u32[]{:S(2)}) %copy-start.3) | copy-done | bytes 4194328
  84.4 10.0 %all_gather.7 = f32[4,64,512]{2,1,0:T(8,128)S(1)} all-gather(f32[1,64,512]{2,1,0:T(8,128)S(1)} %slice.13), channel_id=1, replica_groups=mesh['tm'=4,'paths'=8] {'tm'}, dimensions={0}, use_global_device_ids=true | all-gather | bytes 655360 | tf_op jit(solution)/shard_map/all_gather | solution.py:11
  94.5 10.7 %all_gather.6 = f32[4,64,512]{2,1,0:T(8,128)S(1)} all-gather(f32[1,64,512]{2,1,0:T(8,128)S(1)} %slice.10), channel_id=1, replica_groups=mesh['tm'=4,'paths'=8] {'tm'}, dimensions={0}, use_global_device_ids=true | all-gather | bytes 655360 | tf_op jit(solution)/shard_map/all_gather | solution.py:11
  105.3 0.2 while.12
  105.6 0.0 copy-start.2
  105.6 4.8 %copy.39 = f32[4,8,64,512]{3,1,2,0:T(8,128)S(1)} copy(f32[4,8,64,512]{3,2,1,0:T(8,128)} %bitcast.46) | data formatting | bytes 8388608
  110.4 0.0 copy-done.2
  110.4 0.9 subtract_reduce_fusion
  111.3 7.9 %all_to_all.5 = f32[4,16,512]{2,1,0:T(8,128)S(1)} all-to-all(f32[4,16,512]{2,1,0:T(8,128)S(1)} %reshape.24), channel_id=1, replica_groups=mesh['tm'=4,'paths'=8] {'tm'}, dimensions={0} | all-to-all | bytes 262144 | tf_op jit(solution)/shard_map/all_to_all | solution.py:66
  119.2 0.6 reduce_max.19
  (7 shorter events, 0.1 us)
Async XLA Ops:
  0.0 10.0 %collective-permute-start = (bf16[32,64]{1,0:T(8,128)(2,1)}, bf16[32,64]{1,0:T(8,128)(2,1)S(1)}, u32[]{:S(2)}, u32[]{:S(2)}) collective-permute-start(bf16[32,64]{1,0:T(8,128)(2,1)} %param.5), channel_id=1, source_target_pairs={{0,7},{1,0},{2,1},{3,2},{4,3},{5,4},{6,5},{7,6},{8,15},{9,8},{10,9... | collective-permute-start | bytes 12296 | tf_op jit(solution)/shard_map/ppermute | solution.py:38
  10.0 6.5 %copy-start = (bf16[32,512,256]{2,1,0:T(8,128)(2,1)S(1)}, bf16[32,512,256]{2,1,0:T(8,128)(2,1)}, u32[]{:S(2)}) copy-start(bf16[32,512,256]{2,1,0:T(8,128)(2,1)} %param.4) | copy-start | bytes 25165828
  10.0 6.4 %collective-permute-start.1 = (bf16[32,64]{1,0:T(8,128)(2,1)S(1)}, bf16[32,64]{1,0:T(8,128)(2,1)S(1)}, u32[]{:S(2)}, u32[]{:S(2)}) collective-permute-start(bf16[32,64]{1,0:T(8,128)(2,1)S(1)} %collective-permute-done), channel_id=1, source_target_pairs={{0,7},{1,0},{2,1},{3,2},{4,3},{5,4},{6,5},{7,6},{8,15},{9,8},{10,9... | collective-permute-start | bytes 12296 | tf_op jit(solution)/shard_map/ppermute | solution.py:38
  16.4 3.3 %collective-permute-start.2 = (bf16[32,64]{1,0:T(8,128)(2,1)S(1)}, bf16[32,64]{1,0:T(8,128)(2,1)S(1)}, u32[]{:S(2)}, u32[]{:S(2)}) collective-permute-start(bf16[32,64]{1,0:T(8,128)(2,1)S(1)} %collective-permute-done.1), channel_id=1, source_target_pairs={{0,7},{1,0},{2,1},{3,2},{4,3},{5,4},{6,5},{7,6},{8,15},{9,8},{10,9... | collective-permute-start | bytes 12296 | tf_op jit(solution)/shard_map/ppermute | solution.py:38
  19.7 4.9 %collective-permute-start.3 = (bf16[32,64]{1,0:T(8,128)(2,1)S(1)}, bf16[32,64]{1,0:T(8,128)(2,1)S(1)}, u32[]{:S(2)}, u32[]{:S(2)}) collective-permute-start(bf16[32,64]{1,0:T(8,128)(2,1)S(1)} %collective-permute-done.2), channel_id=1, source_target_pairs={{0,7},{1,0},{2,1},{3,2},{4,3},{5,4},{6,5},{7,6},{8,15},{9,8},{10,9... | collective-permute-start | bytes 12296 | tf_op jit(solution)/shard_map/ppermute | solution.py:38
  24.6 4.9 %collective-permute-start.4 = (bf16[32,64]{1,0:T(8,128)(2,1)S(1)}, bf16[32,64]{1,0:T(8,128)(2,1)S(1)}, u32[]{:S(2)}, u32[]{:S(2)}) collective-permute-start(bf16[32,64]{1,0:T(8,128)(2,1)S(1)} %collective-permute-done.3), channel_id=1, source_target_pairs={{0,7},{1,0},{2,1},{3,2},{4,3},{5,4},{6,5},{7,6},{8,15},{9,8},{10,9... | collective-permute-start | bytes 12296 | tf_op jit(solution)/shard_map/ppermute | solution.py:38
  29.5 4.9 %collective-permute-start.5 = (bf16[32,64]{1,0:T(8,128)(2,1)S(1)}, bf16[32,64]{1,0:T(8,128)(2,1)S(1)}, u32[]{:S(2)}, u32[]{:S(2)}) collective-permute-start(bf16[32,64]{1,0:T(8,128)(2,1)S(1)} %collective-permute-done.4), channel_id=1, source_target_pairs={{0,7},{1,0},{2,1},{3,2},{4,3},{5,4},{6,5},{7,6},{8,15},{9,8},{10,9... | collective-permute-start | bytes 12296 | tf_op jit(solution)/shard_map/ppermute | solution.py:38
  34.4 4.9 %collective-permute-start.6 = (bf16[32,64]{1,0:T(8,128)(2,1)S(1)}, bf16[32,64]{1,0:T(8,128)(2,1)S(1)}, u32[]{:S(2)}, u32[]{:S(2)}) collective-permute-start(bf16[32,64]{1,0:T(8,128)(2,1)S(1)} %collective-permute-done.5), channel_id=1, source_target_pairs={{0,7},{1,0},{2,1},{3,2},{4,3},{5,4},{6,5},{7,6},{8,15},{9,8},{10,9... | collective-permute-start | bytes 12296 | tf_op jit(solution)/shard_map/ppermute | solution.py:38
  58.7 2.8 %copy-start.1 = (f32[32,32768]{1,0:T(8,128)}, f32[32,32768]{1,0:T(8,128)S(1)}, u32[]{:S(2)}) copy-start(f32[32,32768]{1,0:T(8,128)S(1)} %fusion.19) | copy-start | bytes 12582916
  82.5 2.0 %copy-start.3 = (f32[32,64,512]{2,1,0:T(8,128)}, f32[32,64,512]{2,1,0:T(8,128)S(1)}, u32[]{:S(2)}) copy-start(f32[32,64,512]{2,1,0:T(8,128)S(1)} %broadcast_maximum_fusion) | copy-start | bytes 12582916
  105.6 4.8 %copy-start.2 = (f32[32,32768]{1,0:T(8,128)S(1)}, f32[32,32768]{1,0:T(8,128)}, u32[]{:S(2)}) copy-start(f32[32,32768]{1,0:T(8,128)} %copy-done.1) | copy-start | bytes 12582916
